TPU v7x, 256 devices: a whole 4x4x8 slice. The times are simulated.
256 devices in a mesh: dp: 2 (over core), ret: 16 (over y, x), ctx: 8 (over z).
Axes of the slice: x: 4, y: 4, z: 8, core: 2. Of those that a mesh axis runs over, the one named last changes fastest.
Arguments:
- queries: bfloat16 [2, 8192, 4096], P('dp', 'ret', 'ctx'), may hold values from -6 to 6
- enc_states: bfloat16 [2, 32768, 896], P('dp', 'ret'), may hold values from -1600 to 1600
- w_key: bfloat16 [896, 4096], P(None, 'ctx'), may hold values from -0.1875 to 0.1875
- w_value: bfloat16 [896, 4096], P(None, 'ctx'), may hold values from -0.59765625 to 0.59765625
- shard_ids: int32 [2, 128, 2], P('dp', 'ret'), may hold values from 0 to 15, all different within a row; in each aligned block of 8 rows (0 to 7, 8 to 15, ..., all dimensions but the last counted through in order) at most 2 rows name the same one
- row_ids: int32 [2, 128, 2], P('dp', 'ret'), may hold values from 0 to 15
- grad_out: bfloat16 [2, 8192, 4096], P('dp', 'ret', 'ctx'), may hold values from -6 to 6
Outputs:
- attended: bfloat16 [2, 8192, 4096], P('dp', 'ret', 'ctx')
- grad_queries: bfloat16 [2, 8192, 4096], P('dp', 'ret', 'ctx')
- grad_w_key: float32 [896, 4096], P(('dp', 'ret'), 'ctx')
- grad_w_value: float32 [896, 4096], P(('dp', 'ret'), 'ctx')
Inputs may be any that keep to these rules, and one draw needn't show every extreme that they name: `shard_ids`: each block names 2 different shards; among the 8 blocks that one index of ret holds, no shard is named by more than 2 blocks, a bound that some block reaches.
All inputs are finite; a program needn't handle non-finite values.
Results may differ from a plain program's by a relative error of at most 0.019.
Values may be sent and summed in bfloat16 or wider, within the bound.
A program may use at most 128 MiB of HBM per device.

v0:
```python
import math

import jax
import jax.numpy as jnp
from jax import lax
from jax.sharding import PartitionSpec as P

HEAD_DIM = 128
NEIGH_LEN = 128
NEIGHBOURS = 2


def normalize_rows(states):
    floats = states.astype(jnp.float32)
    mean_square = jnp.mean(floats * floats, axis=-1, keepdims=True)
    return (floats * lax.rsqrt(mean_square + 1e-06)).astype(jnp.bfloat16)


def contract_rows(lhs_rows, rhs_rows):
    return lax.dot_general(
        lhs_rows, rhs_rows, (((0,), (0,)), ((), ())), preferred_element_type=jnp.float32
    )


def attend(query_block, key_block, value_block, grad_block):
    score_scale = 1.0 / math.sqrt(HEAD_DIM)
    scores = (
        jnp.einsum("cthd,cjhd->chtj", query_block, key_block, preferred_element_type=jnp.float32)
        * score_scale
    )
    exponent = jnp.exp(scores)
    denominator = jnp.sum(exponent, axis=-1)
    numerator = jnp.einsum(
        "chtj,cjhd->cthd",
        exponent.astype(jnp.bfloat16),
        value_block,
        preferred_element_type=jnp.float32,
    )
    output = numerator / jnp.transpose(denominator, (0, 2, 1))[..., None]
    prob_grad = jnp.einsum(
        "cthd,cjhd->chtj", grad_block, value_block, preferred_element_type=jnp.float32
    )
    row_delta = jnp.transpose(jnp.sum(grad_block.astype(jnp.float32) * output, axis=-1), (0, 2, 1))
    probability = exponent / denominator[..., None]
    score_grad = (probability * (prob_grad - row_delta[..., None]) * score_scale).astype(
        jnp.bfloat16
    )
    grad_query = jnp.einsum(
        "chtj,cjhd->cthd", score_grad, key_block, preferred_element_type=jnp.float32
    ).astype(jnp.bfloat16)
    grad_key = jnp.einsum(
        "chtj,cthd->cjhd", score_grad, query_block, preferred_element_type=jnp.float32
    ).astype(jnp.bfloat16)
    grad_value = jnp.einsum(
        "chtj,cthd->cjhd",
        probability.astype(jnp.bfloat16),
        grad_block,
        preferred_element_type=jnp.float32,
    ).astype(jnp.bfloat16)
    return (output.astype(jnp.bfloat16), grad_query, grad_key, grad_value)


def local(queries, enc_states, w_key, w_value, shard_ids, row_ids, grad_out):
    n_ret = lax.axis_size("ret")
    me_index = lax.axis_index("ret")
    blocks = shard_ids.shape[1]
    request_count = blocks * NEIGHBOURS
    capacity = request_count * 2 // n_ret
    feat_width = queries.shape[2]
    head_count = feat_width // HEAD_DIM
    db_dev = enc_states.shape[1] // NEIGH_LEN
    enc_width = enc_states.shape[2]
    context_rows = NEIGHBOURS * NEIGH_LEN
    every_shard, every_row = (
        lax.all_gather(shard_ids, "ret", axis=1, tiled=True),
        lax.all_gather(row_ids, "ret", axis=1, tiled=True),
    )
    req_shard = every_shard.reshape(n_ret, request_count)
    req_row = every_row.reshape(n_ret, request_count)
    positions = jnp.arange(request_count, dtype=jnp.int32)
    earlier = positions[None, :] < positions[:, None]
    same_shard = req_shard[:, :, None] == req_shard[:, None, :]
    slot_rank = jnp.sum((same_shard & earlier[None]).astype(jnp.int32), axis=2)
    own_shard = shard_ids.reshape(request_count)
    own_same = own_shard[:, None] == own_shard[None, :]
    own_rank = jnp.sum((own_same & earlier).astype(jnp.int32), axis=1)
    own_slot = own_shard * capacity + own_rank
    slot_iota = jnp.arange(capacity, dtype=jnp.int32)
    select = (req_shard[:, None, :] == me_index) & (
        slot_rank[:, None, :] == slot_iota[None, :, None]
    )
    filled = jnp.any(select, axis=2).reshape(-1)
    row_for = jnp.sum(jnp.where(select, req_row[:, None, :], 0), axis=2).reshape(-1)
    normed = normalize_rows(enc_states[0])
    normed_rows = normed.reshape(db_dev, NEIGH_LEN, enc_width)
    query_blocks = queries[0].reshape(blocks, -1, head_count, HEAD_DIM)
    grad_blocks = grad_out[0].reshape(blocks, -1, head_count, HEAD_DIM)
    both_weights = jnp.concatenate([w_key, w_value], axis=1)
    projected = jnp.dot(normed, both_weights, preferred_element_type=jnp.float32).astype(
        jnp.bfloat16
    )
    kv_table = projected.reshape(db_dev, NEIGH_LEN, 2 * feat_width)
    picked = jnp.take(kv_table, row_for, axis=0)
    outgoing = jnp.where(filled[:, None, None], picked, jnp.zeros_like(picked))
    outgoing = outgoing.reshape(n_ret, capacity, NEIGH_LEN, 2 * feat_width)
    incoming = lax.all_to_all(outgoing, "ret", split_axis=0, concat_axis=0, tiled=True)
    own_rows = jnp.take(
        incoming.reshape(n_ret * capacity, NEIGH_LEN, 2 * feat_width), own_slot, axis=0
    )
    own_rows = own_rows.reshape(blocks, context_rows, 2, head_count, HEAD_DIM)
    attended, grad_query, grad_key, grad_value = attend(
        query_blocks, own_rows[:, :, 0], own_rows[:, :, 1], grad_blocks
    )
    returned_grads = jnp.concatenate(
        [
            grad_key.reshape(request_count, NEIGH_LEN, feat_width),
            grad_value.reshape(request_count, NEIGH_LEN, feat_width),
        ],
        axis=2,
    )
    grad_slots = jnp.zeros((n_ret * capacity, NEIGH_LEN, 2 * feat_width), jnp.bfloat16)
    grad_slots = grad_slots.at[own_slot].set(returned_grads)
    arrived = lax.all_to_all(
        grad_slots.reshape(n_ret, capacity, NEIGH_LEN, 2 * feat_width),
        "ret",
        split_axis=0,
        concat_axis=0,
        tiled=True,
    )
    state_rows = jnp.take(normed_rows, row_for, axis=0)
    partial_value = contract_rows(
        state_rows.reshape(-1, enc_width), arrived.reshape(-1, 2 * feat_width)
    )
    summed = lax.psum_scatter(
        partial_value.astype(jnp.bfloat16), ("dp", "ret"), scatter_dimension=0, tiled=True
    ).astype(jnp.float32)
    grad_w_key = summed[:, :feat_width]
    grad_w_value = summed[:, feat_width:]
    return (
        attended.reshape(1, -1, feat_width),
        grad_query.reshape(1, -1, feat_width),
        grad_w_key,
        grad_w_value,
    )


def solution(mesh):
    placed = (
        P("dp", "ret", "ctx"),
        P("dp", "ret", None),
        P(None, "ctx"),
        P(None, "ctx"),
        P("dp", "ret", None),
        P("dp", "ret", None),
        P("dp", "ret", "ctx"),
    )
    return jax.shard_map(
        local,
        mesh=mesh,
        in_specs=placed,
        out_specs=(
            P("dp", "ret", "ctx"),
            P("dp", "ret", "ctx"),
            P(("dp", "ret"), "ctx"),
            P(("dp", "ret"), "ctx"),
        ),
        check_vma=False,
    )
```

profile of v0, /device:TPU:1, one launch (start us, length us, event | category | flops | bytes accessed | tf_op | source)
XLA Modules:
  0.0 476.1 jit_solution(10908282372569557570)
XLA Ops:
  0.7 0.9 copy.67
  1.6 19.3 %all_gather.6 = s32[1,128,2]{2,0,1:T(1,128)S(1)} all-gather(s32[1,8,2]{2,0,1:T(1,128)S(1)} %copy.67), channel_id=1, replica_groups=mesh['dp'=2,'ret'=16,'ctx'=8] {'ret'}, dimensions={1}, use_global_device_ids=true | all-gather | bytes 1088 | tf_op jit(solution)/shard_map/all_gather | solution.py:75
  20.9 0.5 broadcast.197
  21.4 0.8 reduce.7
  22.3 0.4 convert_reduce_fusion
  22.7 0.8 copy.69
  23.5 17.6 %all_gather.7 = s32[1,128,2]{2,0,1:T(1,128)S(1)} all-gather(s32[1,8,2]{2,0,1:T(1,128)S(1)} %copy.69), channel_id=1, replica_groups=mesh['dp'=2,'ret'=16,'ctx'=8] {'ret'}, dimensions={1}, use_global_device_ids=true | all-gather | bytes 1088 | tf_op jit(solution)/shard_map/all_gather | solution.py:76
  41.0 0.8 reduce.6
  41.9 0.1 select_reduce_fusion
  42.1 0.1 copy.71
  42.2 0.1 fusion.25
  42.3 0.1 reshape.212
  42.4 2.8 fusion.1
  45.2 0.1 copy.70
  45.3 0.1 copy.68
  45.4 8.4 %convolution_convert_fusion = bf16[2048,1024]{1,0:T(8,128)(2,1)} fusion(bf16[1,2048,896]{2,1,0:T(8,128)(2,1)} %param.8, f32[2048]{0:T(1024)S(1)} %get-tuple-element.9, bf16[896,512]{1,0:T(8,128)(2,1)S(1)} %copy-done.8, bf16[896,512]{1,0:T(8,128)(2,1)S(1)} %copy-done.9), kind=kOutput, calls=%fused_computation.13 | convolution fusion | flops 3769368576 | bytes 9707520 | tf_op jit(solution)/shard_map/dot_general | solution.py:99
  53.9 7.1 %gather_fusion = bf16[32,128,1024]{2,1,0:T(8,128)(2,1)} fusion(bf16[16,128,1024]{2,1,0:T(8,128)(2,1)} %bitcast.112, s32[1024]{0:T(1024)S(1)} %pad_clamp_fusion.1), kind=kCustom, calls=%fused_computation | custom fusion | bytes 16777344 | tf_op jit(solution)/shard_map/jit(_take)/gather | solution.py:103
  60.9 7.6 %select_select_fusion = bf16[16,2,128,1024]{3,2,1,0:T(8,128)(2,1)} fusion(bf16[16,2,128,1024]{3,2,1,0:T(8,128)(2,1)} %bitcast.111, pred[16,2]{1,0:T(8,128)(4,1)S(1)} %copy.70, pred[16,2]{1,0:T(8,128)(4,1)S(1)} %copy.68), kind=kLoop, calls=%fused_computation.4 | loop fusion | flops 8388608 | bytes 16777280 | tf_op jit(solution)/shard_map/jit(_where)/select_n | solution.py:104
  68.5 5.1 %all-to-all-start = ((bf16[16,2,128,1024]{3,2,1,0:T(8,128)(2,1)}), bf16[16,2,128,1024]{3,2,1,0:T(8,128)(2,1)}, u32[]{:S(2)}, u32[]{:S(2)}) async-start(bf16[16,2,128,1024]{3,2,1,0:T(8,128)(2,1)} %select_select_fusion), calls=%async_computation | async-start | bytes 16777216 | tf_op jit(solution)/shard_map/all_to_all | solution.py:106
  73.7 0.1 reshape.210
  73.7 0.1 copy.72
  73.8 0.1 mul.53
  73.9 0.2 convert_reduce_fusion.1
  74.2 0.1 copy.66
  74.3 0.1 reshape_squeeze.6
  74.4 0.1 reshape_squeeze.7
  74.7 99.4 %all-to-all-done = bf16[16,2,128,1024]{3,2,1,0:T(8,128)(2,1)} async-done(((bf16[16,2,128,1024]{3,2,1,0:T(8,128)(2,1)}), bf16[16,2,128,1024]{3,2,1,0:T(8,128)(2,1)}, u32[]{:S(2)}, u32[]{:S(2)}) %all-to-all-start) | async-done | bytes 8388640 | tf_op jit(solution)/shard_map/all_to_all | solution.py:106
  174.1 6.2 %gather_fusion.1 = bf16[16,128,1024]{2,1,0:T(8,128)(2,1)} fusion(bf16[32,128,1024]{2,1,0:T(8,128)(2,1)} %bitcast.6, s32[1024]{0:T(1024)S(1)} %pad_clamp_fusion), kind=kCustom, calls=%fused_computation.1 | custom fusion | bytes 8388672 | tf_op jit(solution)/shard_map/jit(_take)/gather | solution.py:107
  180.2 7.7 %reshape.255 = bf16[8,256,2,4,128]{4,3,2,1,0:T(4,128)(2,1)} reshape(bf16[16,128,1024]{2,1,0:T(8,128)(2,1)} %gather_fusion.1) | data formatting | bytes 8388608 | tf_op jit(solution)/shard_map/jit(_take)/gather | solution.py:107
  187.9 2.9 copy_select_fusion
  190.9 1.0 bitcast_reduce_fusion
  191.8 2.5 convert_bitcast_fusion
  194.4 1.5 multiply_reduce_fusion
  195.8 1.0 fusion.7
  196.9 0.8 convert_bitcast_fusion.1
  197.6 2.9 copy.82
  200.6 4.1 reshape.217
  204.6 3.3 copy.84
  208.0 2.2 reshape.218
  210.2 4.5 pad_maximum_fusion
  214.7 6.7 %copy.85 = bf16[16,128,1024]{2,1,0:T(8,128)(2,1)} copy(bf16[16,128,1024]{1,0,2:T(8,128)(2,1)} %pad_maximum_fusion) | data formatting | bytes 8388608 | tf_op jit(solution)/shard_map/concatenate | solution.py:114
  221.4 4.3 broadcast.174
  225.7 11.0 %scatter_fusion = bf16[32,128,1024]{2,1,0:T(8,128)(2,1)} fusion(bf16[32,128,1024]{2,1,0:T(8,128)(2,1)} %broadcast.174, s32[16]{0:T(128)S(1)} %fusion.27, bf16[16,128,1024]{2,1,0:T(8,128)(2,1)} %copy.85), kind=kCustom, calls=%fused_computation.3 | custom fusion | bytes 12582976 | tf_op jit(solution)/shard_map/scatter | solution.py:122
  236.6 8.4 %all-to-all-start.1 = ((bf16[16,2,128,1024]{3,2,1,0:T(8,128)(2,1)}), bf16[16,2,128,1024]{3,2,1,0:T(8,128)(2,1)}, u32[]{:S(2)}, u32[]{:S(2)}) async-start(bf16[16,2,128,1024]{3,2,1,0:T(8,128)(2,1)} %bitcast.110), calls=%async_computation.1 | async-start | bytes 16777216 | tf_op jit(solution)/shard_map/all_to_all | solution.py:123
  245.1 0.1 reshape.216
  245.2 4.6 multiply_convert_fusion
  249.8 6.4 %gather_fusion.2 = bf16[32,128,896]{2,1,0:T(8,128)(2,1)} fusion(bf16[16,128,896]{2,1,0:T(8,128)(2,1)} %multiply_convert_fusion, s32[1024]{0:T(1024)S(1)} %pad_clamp_fusion.1), kind=kCustom, calls=%fused_computation.2 | custom fusion | bytes 14680192 | tf_op jit(solution)/shard_map/jit(_take)/gather | solution.py:130
  256.2 0.6 dynamic-slice.4
  257.4 6.8 %broadcast_select_fusion = bf16[32,128,896]{2,1,0:T(8,128)(2,1)} fusion(bf16[32,128,896]{2,1,0:T(8,128)(2,1)} %gather_fusion.2, pred[32]{0:T(512)(128)(4,1)S(1)} %compare_and_fusion), kind=kLoop, calls=%fused_computation.10 | loop fusion | flops 3670016 | bytes 14680096 | tf_op jit(solution)/shard_map/jit(_take)/select_n | solution.py:130
  264.3 98.6 %all-to-all-done.1 = bf16[16,2,128,1024]{3,2,1,0:T(8,128)(2,1)} async-done(((bf16[16,2,128,1024]{3,2,1,0:T(8,128)(2,1)}), bf16[16,2,128,1024]{3,2,1,0:T(8,128)(2,1)}, u32[]{:S(2)}, u32[]{:S(2)}) %all-to-all-start.1) | async-done | bytes 8388640 | tf_op jit(solution)/shard_map/all_to_all | solution.py:123
  362.9 12.3 %convolution_convert_fusion.1 = bf16[896,1024]{1,0:T(8,128)(2,1)S(1)} fusion(bf16[4096,896]{1,0:T(8,128)(2,1)} %bitcast.114, bf16[4096,1024]{1,0:T(8,128)(2,1)} %bitcast.23), kind=kOutput, calls=%fused_computation.34 | convolution fusion | flops 7517110272 | bytes 17563648 | tf_op jit(solution)/shard_map/dot_general | solution.py:20
  375.3 84.0 %fusion = bf16[32,1024]{1,0:T(8,128)(2,1)S(1)} fusion(bf16[896,1024]{1,0:T(8,128)(2,1)S(1)} %convolution_convert_fusion.1), kind=kCustom, calls=%all-reduce-scatter | all-reduce-scatter fusion | flops 1048577 | bytes 1901568
  459.3 2.1 collective-permute-start
  461.4 1.9 collective-permute-start.1
  463.3 1.9 collective-permute-start.2
  465.2 1.9 collective-permute-start.3
  467.1 2.1 fusion.18
  469.2 0.4 copy.79
  469.7 1.0 reshape.215
  470.6 0.4 copy.76
  471.1 1.0 reshape.214
  472.1 2.6 collective-permute-done.3
  474.7 0.7 concatenate.8
  475.4 0.7 fusion.31
  (41 shorter events, 0.6 us)
Async XLA Ops:
  0.6 44.8 %copy-start.8 = (bf16[896,512]{1,0:T(8,128)(2,1)S(1)}, bf16[896,512]{1,0:T(8,128)(2,1)}, u32[]{:S(2)}) copy-start(bf16[896,512]{1,0:T(8,128)(2,1)} %param.10) | copy-start | bytes 2752516
  0.6 44.8 %copy-start.9 = (bf16[896,512]{1,0:T(8,128)(2,1)S(1)}, bf16[896,512]{1,0:T(8,128)(2,1)}, u32[]{:S(2)}) copy-start(bf16[896,512]{1,0:T(8,128)(2,1)} %param.9) | copy-start | bytes 2752516
  68.5 5.1 %copy-start.6 = (s32[1,8,2]{1,2,0:T(2,128)S(1)}, s32[1,8,2]{1,2,0:T(2,128)}, u32[]{:S(2)}) copy-start(s32[1,8,2]{1,2,0:T(2,128)} %param.11) | copy-start | bytes 196
  68.5 5.8 %copy-start.3 = (bf16[1,512,512]{2,1,0:T(8,128)(2,1)S(1)}, bf16[1,512,512]{2,1,0:T(8,128)(2,1)}, u32[]{:S(2)}) copy-start(bf16[1,512,512]{2,1,0:T(8,128)(2,1)} %param.7) | copy-start | bytes 1572868
  68.5 5.9 %copy-start.4 = (bf16[1,512,512]{2,1,0:T(8,128)(2,1)S(1)}, bf16[1,512,512]{2,1,0:T(8,128)(2,1)}, u32[]{:S(2)}) copy-start(bf16[1,512,512]{2,1,0:T(8,128)(2,1)} %param.13) | copy-start | bytes 1572868
  68.5 105.6 %all-to-all-start = ((bf16[16,2,128,1024]{3,2,1,0:T(8,128)(2,1)}), bf16[16,2,128,1024]{3,2,1,0:T(8,128)(2,1)}, u32[]{:S(2)}, u32[]{:S(2)}) async-start(bf16[16,2,128,1024]{3,2,1,0:T(8,128)(2,1)} %select_select_fusion), calls=%async_computation | async-start | bytes 16777216 | tf_op jit(solution)/shard_map/all_to_all | solution.py:106
  74.4 116.4 %copy-start.1 = (bf16[8,64,4,128]{3,2,1,0:T(4,128)(2,1)}, bf16[8,64,4,128]{3,2,1,0:T(4,128)(2,1)S(1)}, u32[]{:S(2)}) copy-start(bf16[8,64,4,128]{3,2,1,0:T(4,128)(2,1)S(1)} %reshape_squeeze.6) | copy-start | bytes 1572868
  190.8 5.0 %copy-start = (bf16[8,256,2,4,128]{4,1,3,0,2:T(8,128)(2,1)}, bf16[8,256,2,4,128]{4,1,3,0,2:T(8,128)(2,1)S(1)}, u32[]{:S(2)}) copy-start(bf16[8,256,2,4,128]{4,1,3,0,2:T(8,128)(2,1)S(1)} %copy_select_fusion) | copy-start | bytes 12582916
  195.8 1.0 copy-start.2
  236.6 126.3 %all-to-all-start.1 = ((bf16[16,2,128,1024]{3,2,1,0:T(8,128)(2,1)}), bf16[16,2,128,1024]{3,2,1,0:T(8,128)(2,1)}, u32[]{:S(2)}, u32[]{:S(2)}) async-start(bf16[16,2,128,1024]{3,2,1,0:T(8,128)(2,1)} %bitcast.110), calls=%async_computation.1 | async-start | bytes 16777216 | tf_op jit(solution)/shard_map/all_to_all | solution.py:123
  249.8 6.4 %copy-start.7 = (u32[256]{0:T(256)S(1)}, u32[256]{0:T(256)}, u32[]{:S(2)}) copy-start(u32[256]{0:T(256)} %constant.73) | copy-start | bytes 3076
  459.3 11.4 %copy-start.5 = (bf16[8,64,4,128]{3,1,2,0:T(8,128)(2,1)S(1)}, bf16[8,64,4,128]{3,1,2,0:T(8,128)(2,1)}, u32[]{:S(2)}) copy-start(bf16[8,64,4,128]{3,1,2,0:T(8,128)(2,1)} %get-tuple-element.5) | copy-start | bytes 1572868
  459.3 15.4 %collective-permute-start = (bf16[32,1024]{1,0:T(8,128)(2,1)S(1)}, bf16[32,1024]{1,0:T(8,128)(2,1)S(1)}, u32[]{:S(2)}, u32[]{:S(2)}) collective-permute-start(bf16[32,1024]{1,0:T(8,128)(2,1)S(1)} %fusion), channel_id=1, source_target_pairs={{0,8},{8,16},{16,24},{24,32},{32,40},{40,48},{48,56},{56,64},{64,7... | collective-permute-start | bytes 196616
  461.4 13.3 %collective-permute-start.1 = (bf16[32,1024]{1,0:T(8,128)(2,1)S(1)}, bf16[32,1024]{1,0:T(8,128)(2,1)S(1)}, u32[]{:S(2)}, u32[]{:S(2)}) collective-permute-start(bf16[32,1024]{1,0:T(8,128)(2,1)S(1)} %fusion), channel_id=1, source_target_pairs={{0,16},{8,24},{16,32},{24,40},{32,48},{40,56},{48,64},{56,72},{64,... | collective-permute-start | bytes 196616
  463.3 11.4 %collective-permute-start.2 = (bf16[32,1024]{1,0:T(8,128)(2,1)S(1)}, bf16[32,1024]{1,0:T(8,128)(2,1)S(1)}, u32[]{:S(2)}, u32[]{:S(2)}) collective-permute-start(bf16[32,1024]{1,0:T(8,128)(2,1)S(1)} %fusion), channel_id=1, source_target_pairs={{0,24},{8,32},{16,40},{24,48},{32,56},{40,64},{48,72},{56,80},{64,... | collective-permute-start | bytes 196616
  465.2 9.5 %collective-permute-start.3 = (bf16[28,1024]{1,0:T(8,128)(2,1)S(1)}, bf16[28,1024]{1,0:T(8,128)(2,1)S(1)}, u32[]{:S(2)}, u32[]{:S(2)}) collective-permute-start(bf16[28,1024]{1,0:T(8,128)(2,1)S(1)} %slice.26), channel_id=1, source_target_pairs={{0,32},{8,40},{16,48},{24,56},{32,64},{40,72},{48,80},{56,88},{64,... | collective-permute-start | bytes 172040
where the time goes:
time: 479 us; the launch traced here: 476 us
  waiting for transfers between devices  201 us (42%)
  blocking collectives  121 us (25%)
  local copies, waits for them, and re-layouts  70.3 us (15%)
  other arithmetic  31.8 us (7%)
  matrix products  29.6 us (6%)
  starting transfers between devices  21.3 us (4%)
    all_to_all x1, waiting for transfers between devices, local(): lax.all_to_all(outgoing, 'ret', split_axis=0, concat_axis=0, tiled=True)  99.4 us
    all_to_all x1, waiting for transfers between devices, local(): lax.all_to_all(grad_slots.reshape(n_ret, capacity, NEIGH_LEN, 2 * feat_wi...  98.6 us
    unnamed x1, blocking collectives  84 us
    all_gather x1, blocking collectives, local(): lax.all_gather(shard_ids, 'ret', axis=1, tiled=True)  19.3 us
    all_gather x1, blocking collectives, local(): lax.all_gather(row_ids, 'ret', axis=1, tiled=True)  17.6 us
    gather x2, local copies, waits for them, and re-layouts, local(): jnp.take(incoming.reshape(n_ret * capacity, NEIGH_LEN, 2 * feat_width), o...  13.9 us
    dot_general x1, matrix products, contract_rows(): lax.dot_general(lhs_rows, rhs_rows, (((0,), (0,)), ((), ())), preferred_e...  12.3 us
    scatter x1, local copies, waits for them, and re-layouts, local(): grad_slots = grad_slots.at[own_slot].set(returned_grads)  11 us
  transfers between devices with their start and end apart: 6, of which 3 were waited for; matrix products, arithmetic and copies ran while one was open for 5% of the time, Pallas kernels for 0%

commit v1 on v0

v1 whole, which is shorter than its diff:
```python
import functools
import math

import jax
import jax.numpy as jnp
from jax import lax
from jax.experimental import pallas as pl
from jax.experimental.pallas import tpu as pltpu
from jax.sharding import PartitionSpec as P

HEAD_DIM = 128
NEIGH_LEN = 128
NEIGHBOURS = 2
CAPACITY = 2
MESH = pl.DeviceIdType.MESH
VMEM_LIMIT = 60 * 1024 * 1024


def normalize_rows(states):
    floats = states.astype(jnp.float32)
    mean_square = jnp.mean(floats * floats, axis=-1, keepdims=True)
    return (floats * lax.rsqrt(mean_square + 1e-06)).astype(jnp.bfloat16)


def gather_kernel(
    n_ret, n_ctx, chunks, shard_ref, row_ref, enc_ref, ctx_ref,
    table, arrived, picks, piece, outbound, landed,
    local_sem, table_send, table_recv, slot_send, slot_recv, ring_send, ring_recv,
):
    me = lax.axis_index("ret")
    plane = lax.axis_index("ctx")
    requests = ctx_ref.shape[1]
    rows = piece.shape[1]
    up, down = lax.rem(plane + 1, n_ctx), lax.rem(plane + n_ctx - 1, n_ctx)

    barrier = pltpu.get_barrier_semaphore()

    @pl.loop(1, n_ret)
    def _(k):
        pl.semaphore_signal(
            barrier, inc=1, device_id={"ret": lax.rem(me + k, n_ret)}, device_id_type=MESH
        )

    for z in (up, down):
        pl.semaphore_signal(barrier, inc=1, device_id={"ctx": z}, device_id_type=MESH)

    fetch = pltpu.make_async_copy(
        enc_ref.at[:, pl.ds(pl.multiple_of(plane * rows, rows), rows), :], piece, local_sem.at[0]
    )
    fetch.start()

    shards = [shard_ref[i // NEIGHBOURS, i % NEIGHBOURS] for i in range(requests)]
    slots = []
    for i in range(requests):
        rank = jnp.int32(0)
        for j in range(i):
            if j // NEIGHBOURS != i // NEIGHBOURS:
                rank = rank + jnp.where(shards[j] == shards[i], 1, 0)
        slots.append(shards[i] * CAPACITY + jnp.minimum(rank, CAPACITY - 1))
    shape = table.shape
    lane = lax.broadcasted_iota(jnp.int32, shape, 2)
    place = lax.broadcasted_iota(jnp.int32, shape, 0) * CAPACITY + lane
    place = jnp.where(lane < CAPACITY, place, -1)
    filled = jnp.zeros(shape, jnp.int32)
    for i in range(requests):
        filled = jnp.where(place == slots[i], row_ref[i // NEIGHBOURS, i % NEIGHBOURS], filled)
    table[...] = filled
    pl.semaphore_wait(barrier, n_ret - 1 + 2)

    def table_copy(k):
        peer = lax.rem(me + k, n_ret)
        return pltpu.make_async_remote_copy(
            table.at[peer], arrived.at[me], table_send.at[k], table_recv.at[k],
            device_id={"ret": peer}, device_id_type=MESH,
        )

    def slot_copy(k):
        peer = lax.rem(me + k, n_ret)
        return pltpu.make_async_remote_copy(
            outbound.at[peer], landed.at[pl.ds(me * CAPACITY, CAPACITY)],
            slot_send.at[k], slot_recv.at[k],
            device_id={"ret": peer}, device_id_type=MESH,
        )

    @pl.loop(1, n_ret)
    def _(k):
        table_copy(k).start()

    fetch.wait()

    @pl.loop(0, piece.shape[0])
    def _(i):
        piece[i] = normalize_rows(piece[i])

    @pl.loop(1, n_ret)
    def _(k):
        table_copy(k).wait()

    arrived[me] = table[me]
    to_scalars = pltpu.make_async_copy(arrived, picks, local_sem.at[1])
    to_scalars.start()
    to_scalars.wait()

    @pl.loop(1, n_ret)
    def _(k):
        peer = lax.rem(me + k, n_ret)
        for c in range(CAPACITY):
            outbound[peer, c] = piece[picks[peer, 0, c]]
        slot_copy(k).start()

    for c in range(CAPACITY):
        landed[me * CAPACITY + c] = piece[picks[me, 0, c]]

    @pl.loop(1, n_ret)
    def _(k):
        slot_copy(k).wait()

    for i in range(requests):
        ctx_ref[plane, i] = landed[slots[i]]

    size = requests // chunks

    def ring_copy(direction, chunk, hop):
        origin = lax.rem(plane + n_ctx - hop, n_ctx) if direction == 0 else lax.rem(plane + hop, n_ctx)
        where = ctx_ref.at[origin, pl.ds(chunk * size, size)]
        return pltpu.make_async_remote_copy(
            where, where,
            ring_send.at[direction, chunk, hop], ring_recv.at[direction, chunk, hop],
            device_id={"ctx": up if direction == 0 else down}, device_id_type=MESH,
        )

    half = n_ctx // 2
    hops = [[half - chunk % 2, n_ctx - 1 - half + chunk % 2] for chunk in range(chunks)]
    for wave in range(chunks + half):
        for chunk in range(chunks):
            hop = wave - chunk
            for direction in range(2):
                if hop >= 1 and hop <= hops[chunk][direction]:
                    ring_copy(direction, chunk, hop - 1).wait_recv()
                if hop >= 0 and hop < hops[chunk][direction]:
                    ring_copy(direction, chunk, hop).start()
    for chunk in range(chunks):
        for direction in range(2):
            for hop in range(hops[chunk][direction]):
                ring_copy(direction, chunk, hop).wait_send()


def gather_context(shard_ids, row_ids, enc, n_ret, n_ctx):
    db_dev, length, width = enc.shape
    requests = shard_ids.shape[0] * NEIGHBOURS
    rows = length // n_ctx
    chunks = 4
    hop_max = n_ctx // 2
    dma = pltpu.SemaphoreType.DMA
    return pl.pallas_call(
        functools.partial(gather_kernel, n_ret, n_ctx, chunks),
        out_shape=jax.ShapeDtypeStruct((n_ctx, requests, rows, width), jnp.bfloat16),
        in_specs=[
            pl.BlockSpec(memory_space=pltpu.SMEM),
            pl.BlockSpec(memory_space=pltpu.SMEM),
            pl.BlockSpec(memory_space=pl.ANY),
        ],
        out_specs=pl.BlockSpec(memory_space=pltpu.VMEM),
        scratch_shapes=[
            pltpu.VMEM((n_ret, 1, 128), jnp.int32),
            pltpu.VMEM((n_ret, 1, 128), jnp.int32),
            pltpu.SMEM((n_ret, 1, 128), jnp.int32),
            pltpu.VMEM((db_dev, rows, width), jnp.bfloat16),
            pltpu.VMEM((n_ret, CAPACITY, rows, width), jnp.bfloat16),
            pltpu.VMEM((n_ret * CAPACITY, rows, width), jnp.bfloat16),
            dma((2,)),
            dma((n_ret,)), dma((n_ret,)),
            dma((n_ret,)), dma((n_ret,)),
            dma((2, chunks, hop_max)), dma((2, chunks, hop_max)),
        ],
        compiler_params=pltpu.CompilerParams(
            collective_id=0, has_side_effects=True, vmem_limit_bytes=VMEM_LIMIT
        ),
    )(shard_ids, row_ids, enc)


def dot_nt(a, b):
    return lax.dot_general(a, b, (((1,), (1,)), ((), ())), preferred_element_type=jnp.float32)


def dot_tn(a, b):
    return lax.dot_general(a, b, (((0,), (0,)), ((), ())), preferred_element_type=jnp.float32)


def dot_nn(a, b):
    return jnp.dot(a, b, preferred_element_type=jnp.float32)


def attend_kernel(
    tokens, ctx_ref, wk_ref, wv_ref, q_ref, g_ref, att_ref, dq_ref, gw_ref, flipped, kv_grad
):
    scale = 1.0 / math.sqrt(HEAD_DIM)
    blocks = q_ref.shape[0] // tokens
    width = ctx_ref.shape[3]
    feat = q_ref.shape[1]
    context = NEIGHBOURS * NEIGH_LEN
    pair = 2 * HEAD_DIM

    def stacked(x):
        lane = lax.broadcasted_iota(jnp.int32, x.shape, 1)
        zero = jnp.zeros_like(x)
        return jnp.concatenate(
            [jnp.where(lane < HEAD_DIM, x, zero), jnp.where(lane >= HEAD_DIM, x, zero)], axis=0
        )

    def unstacked(x):
        return jnp.concatenate([x[:tokens, :HEAD_DIM], x[tokens:, HEAD_DIM:]], axis=1)

    @pl.loop(0, blocks)
    def _(u):
        normed = ctx_ref[:, pl.ds(u * NEIGHBOURS, NEIGHBOURS)].reshape(context, width)
        at = pl.ds(pl.multiple_of(u * context, context), context)
        flipped[:, at] = normed.T
        rows = pl.ds(pl.multiple_of(u * tokens, tokens), tokens)
        for p in range(feat // pair):
            cols = pl.ds(p * pair, pair)
            keys = dot_nn(normed, wk_ref[:, cols]).astype(jnp.bfloat16)
            values = dot_nn(normed, wv_ref[:, cols]).astype(jnp.bfloat16)
            q = stacked(q_ref[rows, cols])
            g = stacked(g_ref[rows, cols])
            expo = jnp.exp(dot_nt(q, keys) * scale)
            inverse = 1.0 / jnp.sum(expo, axis=1, keepdims=True)
            out = dot_nn(expo.astype(jnp.bfloat16), values) * inverse
            att_ref[rows, cols] = unstacked(out).astype(jnp.bfloat16)
            delta = jnp.sum(g.astype(jnp.float32) * out, axis=1, keepdims=True)
            dprob = dot_nt(g, values)
            probs = expo * inverse
            dscore = (probs * (dprob - delta) * scale).astype(jnp.bfloat16)
            dq_ref[rows, cols] = unstacked(dot_nn(dscore, keys)).astype(jnp.bfloat16)
            kv_grad[at, cols] = dot_tn(dscore, q).astype(jnp.bfloat16)
            kv_grad[at, pl.ds(feat + p * pair, pair)] = dot_tn(
                probs.astype(jnp.bfloat16), g
            ).astype(jnp.bfloat16)

    tile = 64

    @pl.loop(0, width // 2 // tile)
    def _(i):
        at = pl.ds(pl.multiple_of(i * tile, tile), tile)
        for part in range(2):
            whole = pl.ds(pl.multiple_of(part * (width // 2) + i * tile, tile), tile)
            gw_ref[part, at, :] = dot_nn(flipped[whole, :], kv_grad[...])


def attend(ctx, w_key, w_value, queries, grad_out, tokens):
    n_ctx, requests, rows, width = ctx.shape
    seq, feat = queries.shape
    vmem = pl.BlockSpec(memory_space=pltpu.VMEM)
    return pl.pallas_call(
        functools.partial(attend_kernel, tokens),
        out_shape=(
            jax.ShapeDtypeStruct((seq, feat), jnp.bfloat16),
            jax.ShapeDtypeStruct((seq, feat), jnp.bfloat16),
            jax.ShapeDtypeStruct((2, width // 2, 2 * feat), jnp.float32),
        ),
        in_specs=[vmem] * 5,
        out_specs=(vmem,) * 3,
        scratch_shapes=[
            pltpu.VMEM((width, requests * NEIGH_LEN), jnp.bfloat16),
            pltpu.VMEM((requests * NEIGH_LEN, 2 * feat), jnp.bfloat16),
        ],
        compiler_params=pltpu.CompilerParams(vmem_limit_bytes=VMEM_LIMIT),
    )(ctx, w_key, w_value, queries, grad_out)


def reduce_kernel(
    n_ret, gw_ref, key_ref, value_ref,
    mine, theirs, summed, parts, landed, pair_sem, send_sem, recv_sem,
):
    me = lax.axis_index("ret")
    core = lax.axis_index("dp")
    _, half, cols = gw_ref.shape
    share = half // n_ret
    feat = cols // 2

    barrier = pltpu.get_barrier_semaphore()

    @pl.loop(1, n_ret)
    def _(k):
        pl.semaphore_signal(
            barrier, inc=1, device_id={"ret": lax.rem(me + k, n_ret)}, device_id_type=MESH
        )

    pl.semaphore_signal(barrier, inc=1, device_id={"dp": 1 - core}, device_id_type=MESH)
    mine[...] = gw_ref[1 - core].astype(jnp.bfloat16)
    pl.semaphore_wait(barrier, n_ret)
    swap = pltpu.make_async_remote_copy(
        mine, theirs, pair_sem.at[0], pair_sem.at[1],
        device_id={"dp": 1 - core}, device_id_type=MESH,
    )
    swap.start()
    swap.wait()

    def copy(k):
        peer = lax.rem(me + k, n_ret)
        return pltpu.make_async_remote_copy(
            parts.at[peer], landed.at[k], send_sem.at[k], recv_sem.at[k],
            device_id={"ret": peer}, device_id_type=MESH,
        )

    summed[...] = gw_ref[core] + theirs[...].astype(jnp.float32)
    for r in range(n_ret):
        parts[r, :share, :] = summed[pl.ds(r * share, share), :].astype(jnp.bfloat16)

    @pl.loop(1, n_ret)
    def _(k):
        copy(k).start()

    landed[0] = parts[me]

    @pl.loop(1, n_ret)
    def _(k):
        copy(k).wait()

    total = landed[0, :share, :].astype(jnp.float32)
    for k in range(1, n_ret):
        total = total + landed[k, :share, :].astype(jnp.float32)
    key_ref[...] = total[:, :feat]
    value_ref[...] = total[:, feat:]


def reduce_grads(gw, n_ret):
    _, half, cols = gw.shape
    share = half // n_ret
    padded = -(-share // 16) * 16
    vmem = pl.BlockSpec(memory_space=pltpu.VMEM)
    dma = pltpu.SemaphoreType.DMA
    return pl.pallas_call(
        functools.partial(reduce_kernel, n_ret),
        out_shape=(jax.ShapeDtypeStruct((share, cols // 2), jnp.float32),) * 2,
        in_specs=[vmem],
        out_specs=(vmem, vmem),
        scratch_shapes=[
            pltpu.VMEM((half, cols), jnp.bfloat16),
            pltpu.VMEM((half, cols), jnp.bfloat16),
            pltpu.VMEM((half, cols), jnp.float32),
            pltpu.VMEM((n_ret, padded, cols), jnp.bfloat16),
            pltpu.VMEM((n_ret, padded, cols), jnp.bfloat16),
            dma((2,)), dma((n_ret,)), dma((n_ret,)),
        ],
        compiler_params=pltpu.CompilerParams(
            collective_id=1, has_side_effects=True, vmem_limit_bytes=VMEM_LIMIT
        ),
    )(gw)


def solution(mesh):
    n_ret, n_ctx = mesh.shape["ret"], mesh.shape["ctx"]

    def local(queries, enc_states, w_key, w_value, shard_ids, row_ids, grad_out):
        enc = enc_states[0].reshape(-1, NEIGH_LEN, enc_states.shape[2])
        tokens = queries.shape[1] // shard_ids.shape[1]
        ctx = gather_context(shard_ids[0], row_ids[0], enc, n_ret, n_ctx)
        attended, grad_queries, gw = attend(ctx, w_key, w_value, queries[0], grad_out[0], tokens)
        grad_key, grad_value = reduce_grads(gw, n_ret)
        return attended[None], grad_queries[None], grad_key, grad_value

    spread = P("dp", "ret", "ctx")
    listed = P("dp", "ret", None)
    return jax.shard_map(
        local,
        mesh=mesh,
        in_specs=(spread, listed, P(None, "ctx"), P(None, "ctx"), listed, listed, spread),
        out_specs=(spread, spread, P(("dp", "ret"), "ctx"), P(("dp", "ret"), "ctx")),
        check_vma=False,
    )
```

time: 479 us -> 135 us (0.28)
  waiting for transfers between devices: 201 us -> 0 us
  Pallas kernels: 0 us -> 128 us
  blocking collectives: 121 us -> 0 us
  local copies, waits for them, and re-layouts: 70.3 us -> 5.64 us
  other arithmetic: 31.8 us -> 0 us
  matrix products: 29.6 us -> 0 us
  starting transfers between devices: 21.3 us -> 0 us
    all_to_all x2 -> x0, waiting for transfers between devices: 198 us -> none  [the longest x1 99.4 us: local(): lax.all_to_all(outgoing, 'ret', split_axis=0, concat_axis=0, tiled=True)]
    pallas_call x0 -> x3, Pallas kernels: none -> 128 us  [the longest x1 68.6 us: gather_context(): pl.pallas_call(functools.partial(gather_kernel, n_ret, n_ctx, chunks), ou...]
    unnamed x1 -> x0, blocking collectives: 84 us -> none
    all_gather x2 -> x0, blocking collectives: 36.9 us -> none  [the longest x1 19.3 us: local(): lax.all_gather(shard_ids, 'ret', axis=1, tiled=True)]
    dot_general x8 -> x0, matrix products: 29.6 us -> none  [the longest x1 12.3 us: contract_rows(): lax.dot_general(lhs_rows, rhs_rows, (((0,), (0,)), ((), ())), preferred_e...]
    gather x4 -> x0, local copies, waits for them, and re-layouts: 27.3 us -> none  [the longest x2 13.9 us: local(): jnp.take(incoming.reshape(n_ret * capacity, NEIGH_LEN, 2 * feat_width), o...]
    select_n x5 -> x0, other arithmetic: 17.3 us -> none  [the longest x1 7.57 us: local(): outgoing = jnp.where(filled[:, None, None], picked, jnp.zeros_like(picked))]
    all_to_all x2 -> x0, starting transfers between devices: 13.5 us -> none  [the longest x1 8.44 us: local(): lax.all_to_all(grad_slots.reshape(n_ret, capacity, NEIGH_LEN, 2 * feat_wi...]
  transfers between devices with their start and end apart: 6 -> 0, of which waited for: 3 -> 0; matrix products, arithmetic and copies ran while one was open for 5% -> 0% of each run, Pallas kernels for 0% -> 0%
where the time goes in v1:
time: 135 us
  Pallas kernels  128 us (95%)
  local copies, waits for them, and re-layouts  5.64 us (4%)
    pallas_call x1, Pallas kernels, gather_context(): pl.pallas_call(functools.partial(gather_kernel, n_ret, n_ctx, chunks), ou...  68.6 us
    pallas_call x1, Pallas kernels, attend(): pl.pallas_call(functools.partial(attend_kernel, tokens), out_shape=(jax.S...  30.9 us
    pallas_call x1, Pallas kernels, reduce_grads(): pl.pallas_call(functools.partial(reduce_kernel, n_ret), out_shape=(jax.Sh...  28.9 us
    unnamed x2, local copies, waits for them, and re-layouts  2.95 us

profile of v1, /device:TPU:1, one launch (start us, length us, event | category | flops | bytes accessed | tf_op | source)
XLA Modules:
  0.0 134.7 jit_solution(7782352163350761820)
XLA Ops:
  0.6 1.3 copy.11.shard_ref
  2.0 1.3 copy.12.row_ref
  3.3 68.6 %shard_map.102.ctx_ref = bf16[8,16,16,896]{3,2,1,0:T(8,128)(2,1)} custom-call(s32[8,2]{1,0:T(8,128)} %copy.11.shard_ref, s32[8,2]{1,0:T(8,128)} %copy.12.row_ref, bf16[16,128,896]{2,1,0:T(8,128)(2,1)} %bitcast.7), custom_call_target="tpu_custom_call" | custom-call | tf_op jit(solution)/shard_map/pallas_call | solution.py:155
  71.9 30.9 %shard_map.103 = (bf16[512,512]{1,0:T(8,128)(2,1)}, bf16[512,512]{1,0:T(8,128)(2,1)}, f32[2,448,1024]{2,1,0:T(8,128)}) custom-call(bf16[8,16,16,896]{3,2,1,0:T(8,128)(2,1)} %shard_map.102.ctx_ref, bf16[896,512]{1,0:T(8,128)(2,1)} %wk_ref.1, bf16[896,512]{1,0:T(8,128)(2,1)} %wv_ref.1, bf16[512,512]{1,0:T(8,128)(2,1)} %bitcast.8, bf16[512,512]{1,0:T(8,128)(2,1)} %bitcast.9), custom_call_target="tpu_custom_call" | custom-call | tf_op jit(solution)/shard_map/pallas_call | solution.py:254
  102.8 28.9 %shard_map.104 = (f32[28,512]{1,0:T(8,128)}, f32[28,512]{1,0:T(8,128)}) custom-call(f32[2,448,1024]{2,1,0:T(8,128)} %get-tuple-element.11.gw_ref), custom_call_target="tpu_custom_call" | custom-call | tf_op jit(solution)/shard_map/pallas_call | solution.py:333
  131.7 1.5 %copy.15 = f32[28,512]{1,0:T(8,128)} copy(f32[28,512]{1,0:T(8,128)} %get-tuple-element.20) | data formatting | bytes 114688
  133.2 1.5 %copy.16 = f32[28,512]{1,0:T(8,128)} copy(f32[28,512]{1,0:T(8,128)} %get-tuple-element.21) | data formatting | bytes 114688

commit v2 on v0

v2 whole, which is shorter than its diff:
```python
import functools
import math

import jax
import jax.numpy as jnp
from jax import lax
from jax.experimental import pallas as pl
from jax.experimental.pallas import tpu as pltpu
from jax.sharding import PartitionSpec as P

HEAD_DIM = 128
NEIGH_LEN = 128
NEIGHBOURS = 2
CAPACITY = 2
MESH = pl.DeviceIdType.MESH
VMEM_LIMIT = 60 * 1024 * 1024
PAIR = 2 * HEAD_DIM
CHUNKS = 4


def normalize_rows(states):
    floats = states.astype(jnp.float32)
    mean_square = jnp.mean(floats * floats, axis=-1, keepdims=True)
    return (floats * lax.rsqrt(mean_square + 1e-06)).astype(jnp.bfloat16)


def dot_nt(a, b):
    return lax.dot_general(a, b, (((1,), (1,)), ((), ())), preferred_element_type=jnp.float32)


def dot_tn(a, b):
    return lax.dot_general(a, b, (((0,), (0,)), ((), ())), preferred_element_type=jnp.float32)


def dot_nn(a, b):
    return jnp.dot(a, b, preferred_element_type=jnp.float32)


def stacked(x):
    lane = lax.broadcasted_iota(jnp.int32, x.shape, 1)
    zero = jnp.zeros_like(x)
    return jnp.concatenate(
        [jnp.where(lane < HEAD_DIM, x, zero), jnp.where(lane >= HEAD_DIM, x, zero)], axis=0
    )


def unstacked(x):
    tokens = x.shape[0] // 2
    return jnp.concatenate([x[:tokens, :HEAD_DIM], x[tokens:, HEAD_DIM:]], axis=1)


def attend_pair(q, g, keys, values):
    scale = 1.0 / math.sqrt(HEAD_DIM)
    q, g = stacked(q), stacked(g)
    expo = jnp.exp(dot_nt(q, keys) * scale)
    inverse = 1.0 / jnp.sum(expo, axis=1, keepdims=True)
    out = dot_nn(expo.astype(jnp.bfloat16), values) * inverse
    delta = jnp.sum(g.astype(jnp.float32) * out, axis=1, keepdims=True)
    probs = expo * inverse
    dscore = (probs * (dot_nt(g, values) - delta) * scale).astype(jnp.bfloat16)
    grad_q = dot_nn(dscore, keys)
    grad_k = dot_tn(dscore, q)
    grad_v = dot_tn(probs.astype(jnp.bfloat16), g)
    return [
        x.astype(jnp.bfloat16) for x in (unstacked(out), unstacked(grad_q), grad_k, grad_v)
    ]


def step_kernel(
    n_ret, n_ctx, shard_ref, row_ref, enc_ref, wk_ref, wv_ref, q_hbm, g_hbm,
    att_ref, dq_ref, gathered,
    table, arrived, picks, piece, outbound, landed, ctx_ref, weights, q_ref, g_ref,
    projected, flipped, kv_grad, mine, theirs, summed, parts,
    local_sem, table_send, table_recv, slot_send, slot_recv, ring_send, ring_recv,
    pair_send, pair_recv, part_send, part_recv,
):
    me = lax.axis_index("ret")
    plane = lax.axis_index("ctx")
    core = lax.axis_index("dp")
    requests, rows, width = ctx_ref.shape[1:]
    feat = q_ref.shape[1]
    context = NEIGHBOURS * NEIGH_LEN
    blocks = requests // NEIGHBOURS
    tokens = q_ref.shape[0] // blocks
    up, down = lax.rem(plane + 1, n_ctx), lax.rem(plane + n_ctx - 1, n_ctx)
    sibling = {"dp": 1 - core}

    def ret_peer(k):
        return lax.rem(me + k, n_ret)

    barrier = pltpu.get_barrier_semaphore()

    @pl.loop(1, n_ret)
    def _(k):
        pl.semaphore_signal(barrier, inc=1, device_id={"ret": ret_peer(k)}, device_id_type=MESH)

    for z in (up, down):
        pl.semaphore_signal(barrier, inc=1, device_id={"ctx": z}, device_id_type=MESH)
    pl.semaphore_signal(barrier, inc=1, device_id=sibling, device_id_type=MESH)

    loads = [
        pltpu.make_async_copy(source, target, local_sem.at[i])
        for i, (source, target) in enumerate((
            (enc_ref.at[:, pl.ds(pl.multiple_of(plane * rows, rows), rows), :], piece),
            (wk_ref, weights.at[:, pl.ds(0, feat)]),
            (wv_ref, weights.at[:, pl.ds(feat, feat)]),
            (q_hbm, q_ref),
            (g_hbm, g_ref),
        ))
    ]
    for load in loads:
        load.start()

    shards = [shard_ref[i % NEIGHBOURS, i // NEIGHBOURS] for i in range(requests)]
    slots = []
    for i in range(requests):
        rank = jnp.int32(0)
        for j in range(i):
            if j // NEIGHBOURS != i // NEIGHBOURS:
                rank = rank + jnp.where(shards[j] == shards[i], 1, 0)
        slots.append(shards[i] * CAPACITY + jnp.minimum(rank, CAPACITY - 1))
    shape = table.shape
    lane = lax.broadcasted_iota(jnp.int32, shape, 2)
    place = lax.broadcasted_iota(jnp.int32, shape, 0) * CAPACITY + lane
    place = jnp.where(lane < CAPACITY, place, -1)
    filled = jnp.zeros(shape, jnp.int32)
    for i in range(requests):
        filled = jnp.where(place == slots[i], row_ref[i % NEIGHBOURS, i // NEIGHBOURS], filled)
    table[...] = filled
    pl.semaphore_wait(barrier, n_ret - 1 + 2 + 1)

    def table_copy(k):
        return pltpu.make_async_remote_copy(
            table.at[ret_peer(k)], arrived.at[me], table_send.at[k], table_recv.at[k],
            device_id={"ret": ret_peer(k)}, device_id_type=MESH,
        )

    def slot_copy(k):
        return pltpu.make_async_remote_copy(
            outbound.at[ret_peer(k)], landed.at[pl.ds(me * CAPACITY, CAPACITY)],
            slot_send.at[k], slot_recv.at[k],
            device_id={"ret": ret_peer(k)}, device_id_type=MESH,
        )

    @pl.loop(1, n_ret)
    def _(k):
        table_copy(k).start()

    loads[0].wait()

    @pl.loop(0, piece.shape[0])
    def _(i):
        piece[i] = normalize_rows(piece[i])

    @pl.loop(1, n_ret)
    def _(k):
        table_copy(k).wait()

    arrived[me] = table[me]
    to_scalars = pltpu.make_async_copy(arrived, picks, local_sem.at[5])
    to_scalars.start()
    to_scalars.wait()

    @pl.loop(1, n_ret)
    def _(k):
        peer = ret_peer(k)
        for c in range(CAPACITY):
            outbound[peer, c] = piece[picks[peer, 0, c]]
        slot_copy(k).start()

    for c in range(CAPACITY):
        landed[me * CAPACITY + c] = piece[picks[me, 0, c]]
    for load in loads[1:]:
        load.wait()

    @pl.loop(1, n_ret)
    def _(k):
        slot_copy(k).wait()

    for i in range(requests):
        ctx_ref[plane, i] = landed[slots[i]]

    size = requests // CHUNKS

    def ring_copy(direction, chunk, hop):
        step = n_ctx - hop if direction == 0 else hop
        where = ctx_ref.at[lax.rem(plane + step, n_ctx), pl.ds(chunk * size, size)]
        return pltpu.make_async_remote_copy(
            where, where,
            ring_send.at[direction, chunk, hop], ring_recv.at[direction, chunk, hop],
            device_id={"ctx": up if direction == 0 else down}, device_id_type=MESH,
        )

    def compute(chunk):
        first = chunk * size // NEIGHBOURS
        count = size // NEIGHBOURS
        normed = jnp.concatenate([
            ctx_ref[:, (first + b) * NEIGHBOURS : (first + b + 1) * NEIGHBOURS].reshape(context, width)
            for b in range(count)
        ])
        flipped[:, :, pl.ds(first * context, count * context)] = normed.T.reshape(
            2, width // 2, count * context
        )
        for p in range(2 * feat // PAIR):
            cols = pl.ds(p * PAIR, PAIR)
            projected[:, cols] = dot_nn(normed, weights[:, cols]).astype(jnp.bfloat16)
        for b in range(count):
            here = pl.ds(b * context, context)
            at = pl.ds((first + b) * context, context)
            own = pl.ds((first + b) * tokens, tokens)
            for p in range(feat // PAIR):
                cols, late = pl.ds(p * PAIR, PAIR), pl.ds(feat + p * PAIR, PAIR)
                att_ref[own, cols], dq_ref[own, cols], kv_grad[at, cols], kv_grad[at, late] = (
                    attend_pair(
                        q_ref[own, cols], g_ref[own, cols],
                        projected[here, cols], projected[here, late],
                    )
                )

    half = n_ctx // 2
    hops = [[half - chunk % 2, n_ctx - 1 - half + chunk % 2] for chunk in range(CHUNKS)]
    for wave in range(CHUNKS + half):
        for chunk in range(CHUNKS):
            hop = wave - chunk
            for direction in range(2):
                if hop >= 1 and hop <= hops[chunk][direction]:
                    ring_copy(direction, chunk, hop - 1).wait_recv()
                if hop >= 0 and hop < hops[chunk][direction]:
                    ring_copy(direction, chunk, hop).start()
        if wave >= half:
            compute(wave - half)
    for chunk in range(CHUNKS):
        for direction in range(2):
            for hop in range(hops[chunk][direction]):
                ring_copy(direction, chunk, hop).wait_send()

    tiles = 2 * feat // PAIR
    share = width // 2 // n_ret

    def pair_copy(n):
        return pltpu.make_async_remote_copy(
            mine.at[n], theirs.at[n], pair_send.at[n], pair_recv.at[n],
            device_id=sibling, device_id_type=MESH,
        )

    def part_copy(n, k):
        return pltpu.make_async_remote_copy(
            parts.at[n, ret_peer(k)], gathered.at[n, k], part_send.at[n, k], part_recv.at[n, k],
            device_id={"ret": ret_peer(k)}, device_id_type=MESH,
        )

    for n in range(tiles):
        mine[n] = dot_nn(flipped[1 - core], kv_grad[:, pl.ds(n * PAIR, PAIR)]).astype(jnp.bfloat16)
        pair_copy(n).start()
    for n in range(tiles):
        own = dot_nn(flipped[core], kv_grad[:, pl.ds(n * PAIR, PAIR)])
        pair_copy(n).wait()
        summed[...] = own + theirs[n].astype(jnp.float32)
        for r in range(n_ret):
            parts[n, r, :share, :] = summed[pl.ds(r * share, share), :].astype(jnp.bfloat16)

        @pl.loop(1, n_ret)
        def _(k):
            part_copy(n, k).start()

        gathered[n, 0] = parts[n, me]

    @pl.loop(1, n_ret)
    def _(k):
        for n in range(tiles):
            part_copy(n, k).wait()


def step(shard_ids, row_ids, enc, w_key, w_value, queries, grad_out, n_ret, n_ctx):
    db_dev, length, width = enc.shape
    requests = shard_ids.shape[0] * shard_ids.shape[1]
    seq, feat = queries.shape
    rows = length // n_ctx
    half = width // 2
    padded = -(-half // n_ret // 16) * 16
    tiles = 2 * feat // PAIR
    hop_max = n_ctx // 2
    dma = pltpu.SemaphoreType.DMA
    bf16, vmem = jnp.bfloat16, pltpu.VMEM
    smem_spec = pl.BlockSpec(memory_space=pltpu.SMEM)
    any_spec = pl.BlockSpec(memory_space=pl.ANY)
    vmem_spec = pl.BlockSpec(memory_space=pltpu.VMEM)
    return pl.pallas_call(
        functools.partial(step_kernel, n_ret, n_ctx),
        out_shape=(
            jax.ShapeDtypeStruct((seq, feat), bf16),
            jax.ShapeDtypeStruct((seq, feat), bf16),
            jax.ShapeDtypeStruct((tiles, n_ret, padded, PAIR), bf16),
        ),
        in_specs=[smem_spec] * 2 + [any_spec] * 5,
        out_specs=(vmem_spec,) * 3,
        scratch_shapes=[
            vmem((n_ret, 1, 128), jnp.int32),
            vmem((n_ret, 1, 128), jnp.int32),
            pltpu.SMEM((n_ret, 1, 128), jnp.int32),
            vmem((db_dev, rows, width), bf16),
            vmem((n_ret, CAPACITY, rows, width), bf16),
            vmem((n_ret * CAPACITY, rows, width), bf16),
            vmem((n_ctx, requests, rows, width), bf16),
            vmem((width, 2 * feat), bf16),
            vmem((seq, feat), bf16),
            vmem((seq, feat), bf16),
            vmem((requests // CHUNKS * NEIGH_LEN, 2 * feat), bf16),
            vmem((2, half, requests * NEIGH_LEN), bf16),
            vmem((requests * NEIGH_LEN, 2 * feat), bf16),
            vmem((tiles, half, PAIR), bf16),
            vmem((tiles, half, PAIR), bf16),
            vmem((half, PAIR), jnp.float32),
            vmem((tiles, n_ret, padded, PAIR), bf16),
            dma((6,)),
            dma((n_ret,)), dma((n_ret,)),
            dma((n_ret,)), dma((n_ret,)),
            dma((2, CHUNKS, hop_max)), dma((2, CHUNKS, hop_max)),
            dma((tiles,)), dma((tiles,)),
            dma((tiles, n_ret)), dma((tiles, n_ret)),
        ],
        compiler_params=pltpu.CompilerParams(
            collective_id=0, has_side_effects=True, vmem_limit_bytes=VMEM_LIMIT
        ),
    )(shard_ids, row_ids, enc, w_key, w_value, queries, grad_out)


def finish_kernel(att_in, dq_in, gathered, att_ref, dq_ref, key_ref, value_ref):
    att_ref[...] = att_in[...]
    dq_ref[...] = dq_in[...]
    tiles, n_ret, _, cols = gathered.shape
    share = key_ref.shape[0]
    for n in range(tiles):
        total = gathered[n, 0, :share, :].astype(jnp.float32)
        for k in range(1, n_ret):
            total = total + gathered[n, k, :share, :].astype(jnp.float32)
        target = key_ref if n < tiles // 2 else value_ref
        target[:, pl.ds(n % (tiles // 2) * cols, cols)] = total


def finish(attended, grad_queries, gathered, share):
    vmem = pl.BlockSpec(memory_space=pltpu.VMEM)
    tiles, _, _, cols = gathered.shape
    grad = jax.ShapeDtypeStruct((share, tiles // 2 * cols), jnp.float32)
    like = jax.ShapeDtypeStruct(attended.shape, attended.dtype)
    return pl.pallas_call(
        finish_kernel,
        out_shape=(like, like, grad, grad),
        in_specs=[vmem] * 3,
        out_specs=(vmem,) * 4,
    )(attended, grad_queries, gathered)


def solution(mesh):
    n_ret, n_ctx = mesh.shape["ret"], mesh.shape["ctx"]

    def local(queries, enc_states, w_key, w_value, shard_ids, row_ids, grad_out):
        width = enc_states.shape[2]
        enc = enc_states[0].reshape(-1, NEIGH_LEN, width)
        attended, grad_queries, gathered = step(
            shard_ids[0].T, row_ids[0].T, enc, w_key, w_value, queries[0], grad_out[0], n_ret, n_ctx
        )
        attended, grad_queries, grad_key, grad_value = finish(
            attended, grad_queries, gathered, width // (2 * n_ret)
        )
        return attended[None], grad_queries[None], grad_key, grad_value

    spread = P("dp", "ret", "ctx")
    listed = P("dp", "ret", None)
    return jax.shard_map(
        local,
        mesh=mesh,
        in_specs=(spread, listed, P(None, "ctx"), P(None, "ctx"), listed, listed, spread),
        out_specs=(spread, spread, P(("dp", "ret"), "ctx"), P(("dp", "ret"), "ctx")),
        check_vma=False,
    )
```

time: 479 us -> 98.5 us (0.21)
  waiting for transfers between devices: 201 us -> 0 us
  blocking collectives: 121 us -> 0 us
  Pallas kernels: 0 us -> 96.2 us
  local copies, waits for them, and re-layouts: 70.3 us -> 0 us
  other arithmetic: 31.8 us -> 0 us
  matrix products: 29.6 us -> 0 us
  starting transfers between devices: 21.3 us -> 0 us
    all_to_all x2 -> x0, waiting for transfers between devices: 198 us -> none  [the longest x1 99.4 us: local(): lax.all_to_all(outgoing, 'ret', split_axis=0, concat_axis=0, tiled=True)]
    pallas_call x0 -> x2, Pallas kernels: none -> 96.2 us  [the longest x1 93.6 us: step(): pl.pallas_call(functools.partial(step_kernel, n_ret, n_ctx), out_shape=(j...]
    unnamed x1 -> x0, blocking collectives: 84 us -> none
    all_gather x2 -> x0, blocking collectives: 36.9 us -> none  [the longest x1 19.3 us: local(): lax.all_gather(shard_ids, 'ret', axis=1, tiled=True)]
    dot_general x8 -> x0, matrix products: 29.6 us -> none  [the longest x1 12.3 us: contract_rows(): lax.dot_general(lhs_rows, rhs_rows, (((0,), (0,)), ((), ())), preferred_e...]
    gather x4 -> x0, local copies, waits for them, and re-layouts: 27.3 us -> none  [the longest x2 13.9 us: local(): jnp.take(incoming.reshape(n_ret * capacity, NEIGH_LEN, 2 * feat_width), o...]
    select_n x5 -> x0, other arithmetic: 17.3 us -> none  [the longest x1 7.57 us: local(): outgoing = jnp.where(filled[:, None, None], picked, jnp.zeros_like(picked))]
    all_to_all x2 -> x0, starting transfers between devices: 13.5 us -> none  [the longest x1 8.44 us: local(): lax.all_to_all(grad_slots.reshape(n_ret, capacity, NEIGH_LEN, 2 * feat_wi...]
  transfers between devices with their start and end apart: 6 -> 0, of which waited for: 3 -> 0; matrix products, arithmetic and copies ran while one was open for 5% -> 0% of each run, Pallas kernels for 0% -> 0%
where the time goes in v2:
time: 98.5 us; the launch traced here: 96.9 us
  Pallas kernels  96.2 us (98%)
    pallas_call x1, Pallas kernels, step(): pl.pallas_call(functools.partial(step_kernel, n_ret, n_ctx), out_shape=(j...  93.6 us
    pallas_call x1, Pallas kernels, finish(): pl.pallas_call(finish_kernel, out_shape=(like, like, grad, grad), in_spec...  2.58 us

profile of v2, /device:TPU:1, one launch (start us, length us, event | category | flops | bytes accessed | tf_op | source)
XLA Modules:
  0.0 96.9 jit_solution(10643671330766552369)
XLA Ops:
  0.6 93.6 %shard_map.102 = (bf16[512,512]{1,0:T(8,128)(2,1)}, bf16[512,512]{1,0:T(8,128)(2,1)}, bf16[4,16,32,256]{3,2,1,0:T(8,128)(2,1)}) custom-call(s32[2,8]{1,0:T(2,128)} %bitcast.14, s32[2,8]{1,0:T(2,128)} %bitcast.15, bf16[16,128,896]{2,1,0:T(8,128)(2,1)} %bitcast.11, bf16[896,512]{1,0:T(8,128)(2,1)} %wk_ref.1, bf16[896,512]{1,0:T(8,128)(2,1)} %wv_ref.1, ...), custom_call_target="tpu_custom_call" | custom-call | tf_op jit(solution)/shard_map/pallas_call | solution.py:288
  94.3 2.6 %shard_map.103 = (bf16[512,512]{1,0:T(8,128)(2,1)}, bf16[512,512]{1,0:T(8,128)(2,1)}, f32[28,512]{1,0:T(8,128)}, f32[28,512]{1,0:T(8,128)}) custom-call(bf16[512,512]{1,0:T(8,128)(2,1)} %get-tuple-element.11.att_in, bf16[512,512]{1,0:T(8,128)(2,1)} %get-tuple-element.12.dq_in, bf16[4,16,32,256]{3,2,1,0:T(8,128)(2,1)} %get-tuple-element.13.gathered), custom_call_target="tpu_custom_call" | custom-call | tf_op jit(solution)/shard_map/pallas_call | solution.py:346
